TPU v7x, 32 devices: a whole 2x2x4 slice. The times are simulated.
32 devices in a mesh: amp: 32 (over z, y, x, core).
Axes of the slice: x: 2, y: 2, z: 4, core: 2. Of those that a mesh axis runs over, the one named last changes fastest.
Arguments:
- ket_state: float32 [2, 1048576], P(None, 'amp'), may hold values from -6 to 6
- observable: float32 [1048576], P('amp'), may hold values from -6 to 6
- angles: float32 [2, 3], replicated, may hold values from -3.140625 to 3.140625
- gate_kinds: int32 [2, 32], replicated, may hold values from 0 to 2
Outputs:
- bra_state: float32 [2, 1048576], P(None, 'amp')
- grads: float32 [2, 3], replicated
Inputs may be any that keep to these rules, and one draw needn't show every extreme that they name: `gate_kinds`: 0 and 1 name rotations about Y with angles[l, 0] and angles[l, 1], 2 a rotation about Z with angles[l, 2]; entries for qubits at or above the number of qubits are not used.
All inputs are finite; a program needn't handle non-finite values.
Results may differ from a plain program's by a relative error of at most 0.0003.
Values sent between devices are 32-bit elements; how exact they have to be, the bound alone decides.
A program may use at most 128 MiB of HBM per device.

v0:
```python
import functools
import math

import jax
import jax.numpy as jnp
import numpy as np
from jax import lax
from jax.experimental import pallas as pl
from jax.experimental.pallas import tpu as pltpu
from jax.sharding import PartitionSpec as P

MESH = pl.DeviceIdType.MESH
LANE, SUB, MAJOR, DEVICE = range(4)
LANE_BITS, SUB_BITS = 7, 3


def from_partner(value, axis, apart):
    mask = 2**apart
    pairs = [(source, source ^ mask) for source in range(lax.axis_size(axis))]
    return lax.ppermute(value, axis, pairs)


def pair_tables():
    column = np.arange(128)
    flips = []
    signs = []
    for position in range(7):
        upper = column >> position & 1
        flip_table = np.zeros((128, 128), np.float32)
        flip_table[column, column ^ 1 << position] = np.where(upper == 0, -0.5, 0.5)
        flips.append(flip_table)
        signs.append((1 - 2 * upper).astype(np.float32))
    return (np.stack(flips), np.stack(signs))


def layout_map(local_bits, global_bits):
    local_map = list(range(local_bits))
    device_map = [local_bits + bit_num for bit_num in range(global_bits)]
    return (local_map, device_map)


def entangle_sign(local_bits, global_bits, device_id, amp_count):
    local_map, device_map = layout_map(local_bits, global_bits)
    amp_index = lax.iota(jnp.int32, amp_count)
    bit_values = [None] * (local_bits + global_bits)
    for position in range(local_bits):
        bit_values[local_map[position]] = amp_index >> position & 1
    for bit_num in range(global_bits):
        bit_values[device_map[bit_num]] = device_id >> bit_num & 1
    all_bits = local_bits + global_bits
    parity = jnp.zeros((amp_count,), jnp.int32)
    for qubit_id in range(all_bits):
        parity = parity + bit_values[qubit_id] * bit_values[(qubit_id + 1) % all_bits]
    return (1 - 2 * (parity & 1)).astype(jnp.float32)


def rotation_of(angles, gate_kinds, layer_id, qubit_id):
    kind_id = gate_kinds[layer_id, qubit_id]
    chosen = jnp.arange(angles.shape[1]) == kind_id
    rotation = jnp.sum(jnp.where(chosen, angles[layer_id], 0.0))
    return (kind_id, jnp.cos(0.5 * rotation), jnp.sin(0.5 * rotation))


def kind_vector(kind_id, kind_count):
    return (jnp.arange(kind_count) == kind_id).astype(jnp.float32)


def rotate_phase(values, cosine, sine_value):
    return jnp.stack(
        [cosine * values[0] - sine_value * values[1], cosine * values[1] + sine_value * values[0]]
    )


def rotate_position(ket_state, bra_state, position, qubit_id, layer_id, angles, gate_kinds):
    amp_count = ket_state.shape[1]
    fold_shape = (2, amp_count >> position + 1, 2, 1 << position)
    kind_id, cosine, sine_value = rotation_of(angles, gate_kinds, layer_id, qubit_id)

    def turn_y(operands):
        folded_ket, folded_bra = operands
        ket_low, ket_high = (folded_ket[:, :, 0], folded_ket[:, :, 1])
        bra_low, bra_high = (folded_bra[:, :, 0], folded_bra[:, :, 1])
        partial_value = 0.5 * jnp.sum(bra_high * ket_low - bra_low * ket_high)
        new_ket = jnp.stack(
            [cosine * ket_low + sine_value * ket_high, cosine * ket_high - sine_value * ket_low],
            axis=2,
        )
        new_bra = jnp.stack(
            [cosine * bra_low + sine_value * bra_high, cosine * bra_high - sine_value * bra_low],
            axis=2,
        )
        return (new_ket, new_bra, partial_value)

    def turn_z(operands):
        folded_ket, folded_bra = operands
        ket_low, ket_high = (folded_ket[:, :, 0], folded_ket[:, :, 1])
        bra_low, bra_high = (folded_bra[:, :, 0], folded_bra[:, :, 1])
        partial_value = 0.5 * (
            jnp.sum(bra_low[0] * ket_low[1] - bra_low[1] * ket_low[0])
            - jnp.sum(bra_high[0] * ket_high[1] - bra_high[1] * ket_high[0])
        )
        new_ket = jnp.stack(
            [
                rotate_phase(ket_low, cosine, sine_value),
                rotate_phase(ket_high, cosine, -sine_value),
            ],
            axis=2,
        )
        new_bra = jnp.stack(
            [
                rotate_phase(bra_low, cosine, sine_value),
                rotate_phase(bra_high, cosine, -sine_value),
            ],
            axis=2,
        )
        return (new_ket, new_bra, partial_value)

    new_ket, new_bra, partial_value = lax.cond(
        kind_id == 2, turn_z, turn_y, (ket_state.reshape(fold_shape), bra_state.reshape(fold_shape))
    )
    terms = partial_value * kind_vector(kind_id, angles.shape[1])
    return (new_ket.reshape(2, amp_count), new_bra.reshape(2, amp_count), terms)


def contract_rows(left, right):
    return lax.dot_general(
        left,
        right,
        (((0,), (0,)), ((), ())),
        precision=lax.Precision.HIGHEST,
        preferred_element_type=jnp.float32,
    )


def contract_cols(left, right):
    return lax.dot_general(
        left,
        right,
        (((1,), (1,)), ((), ())),
        precision=lax.Precision.HIGHEST,
        preferred_element_type=jnp.float32,
    )


def low_block(ket_state, bra_state, qubit_list, layer_id, angles, gate_kinds):
    amp_count = ket_state.shape[1]
    row_count = amp_count // 128
    flips, signs = pair_tables()
    ket_real = ket_state[0].reshape(row_count, 128)
    ket_imag = ket_state[1].reshape(row_count, 128)
    bra_real = bra_state[0].reshape(row_count, 128)
    bra_imag = bra_state[1].reshape(row_count, 128)
    gram_real = contract_rows(bra_real, ket_real) + contract_rows(bra_imag, ket_imag)
    gram_imag = contract_rows(bra_real, ket_imag) - contract_rows(bra_imag, ket_real)
    gram_diag = jnp.diagonal(gram_imag)
    terms = jnp.zeros((angles.shape[1],), jnp.float32)
    kron_real = None
    kron_imag = None
    for position in range(7):
        kind_id, cosine, sine_value = rotation_of(
            angles, gate_kinds, layer_id, qubit_list[position]
        )
        is_z = kind_id == 2
        partial_value = jnp.where(
            is_z, 0.5 * jnp.sum(signs[position] * gram_diag), jnp.sum(flips[position] * gram_real)
        )
        terms = terms + partial_value * kind_vector(kind_id, angles.shape[1])
        mat_y = jnp.stack([jnp.stack([cosine, sine_value]), jnp.stack([-sine_value, cosine])])
        zero_value = jnp.zeros_like(cosine)
        mat_zr = jnp.stack([jnp.stack([cosine, zero_value]), jnp.stack([zero_value, cosine])])
        mat_zi = jnp.stack(
            [jnp.stack([sine_value, zero_value]), jnp.stack([zero_value, -sine_value])]
        )
        mat_real = jnp.where(is_z, mat_zr, mat_y)
        mat_imag = jnp.where(is_z, mat_zi, jnp.zeros_like(mat_zi))
        if kron_real is None:
            kron_real, kron_imag = (mat_real, mat_imag)
        else:
            kron_real, kron_imag = (
                jnp.kron(mat_real, kron_real) - jnp.kron(mat_imag, kron_imag),
                jnp.kron(mat_real, kron_imag) + jnp.kron(mat_imag, kron_real),
            )

    def apply_block(real_rows, imag_rows):
        new_real = contract_cols(real_rows, kron_real) - contract_cols(imag_rows, kron_imag)
        new_imag = contract_cols(imag_rows, kron_real) + contract_cols(real_rows, kron_imag)
        return jnp.stack([new_real.reshape(amp_count), new_imag.reshape(amp_count)])

    return (apply_block(ket_real, ket_imag), apply_block(bra_real, bra_imag), terms)


def rotate_global(
    ket_state,
    bra_state,
    far_ket,
    far_bra,
    bit_num,
    qubit_id,
    device_id,
    layer_id,
    angles,
    gate_kinds,
):
    kind_id, cosine, sine_value = rotation_of(angles, gate_kinds, layer_id, qubit_id)
    orient = (1 - 2 * (device_id >> bit_num & 1)).astype(jnp.float32)

    def turn_y(operands):
        own_ket, own_bra, other_ket, other_bra = operands
        partial_value = 0.25 * orient * jnp.sum(other_bra * own_ket - own_bra * other_ket)
        return (
            cosine * own_ket + orient * sine_value * other_ket,
            cosine * own_bra + orient * sine_value * other_bra,
            partial_value,
        )

    def turn_z(operands):
        own_ket, own_bra, other_ket, other_bra = operands
        partial_value = 0.5 * orient * jnp.sum(own_bra[0] * own_ket[1] - own_bra[1] * own_ket[0])
        return (
            rotate_phase(own_ket, cosine, orient * sine_value),
            rotate_phase(own_bra, cosine, orient * sine_value),
            partial_value,
        )

    new_ket, new_bra, partial_value = lax.cond(
        kind_id == 2, turn_z, turn_y, (ket_state, bra_state, far_ket, far_bra)
    )
    return (new_ket, new_bra, partial_value * kind_vector(kind_id, angles.shape[1]))


def on_device(ket_state, observable, angles, gate_kinds):
    amp_count = ket_state.shape[1]
    local_bits = amp_count.bit_length() - 1
    group_size = lax.axis_size("amp")
    global_bits = group_size.bit_length() - 1
    device_id = lax.axis_index("amp")
    layer_count = angles.shape[0]
    kind_count = angles.shape[1]
    bra_state = 2.0 / math.sqrt(amp_count * group_size) * observable[None, :] * ket_state
    sign_cache = {}
    grads_local = jnp.zeros((layer_count, kind_count), jnp.float32)
    for sweep_id in range(layer_count):
        layer_id = layer_count - 1 - sweep_id
        layout = 0
        local_map, device_map = layout_map(local_bits, global_bits)
        if layout not in sign_cache:
            sign_cache[layout] = entangle_sign(local_bits, global_bits, device_id, amp_count)
        phase_sign = sign_cache[layout]
        ket_state = ket_state * phase_sign[None, :]
        bra_state = bra_state * phase_sign[None, :]
        ket_state, bra_state, layer_terms = low_block(
            ket_state, bra_state, local_map[:7], layer_id, angles, gate_kinds
        )
        for position in range(7, local_bits):
            ket_state, bra_state, partial_value = rotate_position(
                ket_state, bra_state, position, local_map[position], layer_id, angles, gate_kinds
            )
            layer_terms = layer_terms + partial_value
        for bit_num in range(global_bits):
            far_ket, far_bra = from_partner((ket_state, bra_state), "amp", bit_num)
            ket_state, bra_state, partial_value = rotate_global(
                ket_state,
                bra_state,
                far_ket,
                far_bra,
                bit_num,
                device_map[bit_num],
                device_id,
                layer_id,
                angles,
                gate_kinds,
            )
            layer_terms = layer_terms + partial_value
        grads_local = grads_local.at[layer_id].set(layer_terms)
    grads = lax.psum(grads_local, "amp")
    return (bra_state, grads)


def layouts(major_bits, global_bits):
    low = LANE_BITS + SUB_BITS
    local_bits = low + major_bits
    home, away = {}, {}
    for q in range(LANE_BITS):
        home[q] = away[q] = (LANE, q)
    home[LANE_BITS] = away[LANE_BITS] = (SUB, 0)
    for bit, q in ((1, local_bits - 2), (2, local_bits - 1)):
        home[q] = away[q] = (SUB, bit)
    moved = list(range(low, local_bits - 2)) + [low - 2, low - 1]
    for bit, q in enumerate(moved):
        home[q], away[q] = (MAJOR, bit), (DEVICE, bit)
    for bit in range(global_bits):
        home[local_bits + bit], away[local_bits + bit] = (DEVICE, bit), (MAJOR, bit)
    return home, away


def split_major(x, bit):
    fold = x.reshape((x.shape[0] >> bit + 1, 2, 1 << bit) + x.shape[1:])
    return fold[:, 0], fold[:, 1]


def join_major(x0, x1):
    out = jnp.stack([x0, x1], axis=1)
    return out.reshape((-1,) + out.shape[3:])


def minor_bit(axis, bit):
    return lax.broadcasted_iota(jnp.int32, (1, 8, 128), 1 if axis == SUB else 2) >> bit & 1


def minor_sign(axis, bit):
    return (1 - 2 * minor_bit(axis, bit)).astype(jnp.float32)


def shifted(x, axis, by):
    dim = 1 if axis == SUB else 2
    return pltpu.roll(x, by % x.shape[dim], dim)


def partner(x, axis, bit):
    step = 1 << bit
    up = shifted(x, axis, -step)
    if 2 * step == x.shape[1 if axis == SUB else 2]:
        return up
    return jnp.where(minor_bit(axis, bit) == 0, up, shifted(x, axis, step))


def swap_bits(x, major, sub):
    x0, x1 = split_major(x, major)
    lower = minor_bit(SUB, sub) == 0

    def roll3(y, by):
        z = y.reshape((-1,) + y.shape[2:])
        return shifted(z, SUB, by).reshape(y.shape)

    step = 1 << sub
    return join_major(jnp.where(lower, x0, roll3(x1, step)), jnp.where(lower, roll3(x0, -step), x1))


def gate(state, place, coef):
    re, im = state
    axis, bit = place
    c, sy, sz = coef
    if axis == MAJOR:
        r0, r1 = split_major(re, bit)
        i0, i1 = split_major(im, bit)
        return (
            join_major(c * r0 + sy * r1 - sz * i0, c * r1 - sy * r0 + sz * i1),
            join_major(c * i0 + sy * i1 + sz * r0, c * i1 - sy * i0 - sz * r1),
        )
    z = minor_sign(axis, bit)
    zy, zz = sy * z, sz * z
    return (
        c * re + zy * partner(re, axis, bit) - zz * im,
        c * im + zy * partner(im, axis, bit) + zz * re,
    )


def lane_matrix(coefs):
    at = [lax.broadcasted_iota(jnp.int32, (128, 128), d) for d in range(2)]
    re, im = None, None
    for bit, (c, sy, sz) in enumerate(coefs):
        old, new = (x >> bit & 1 for x in at)
        z = (1 - 2 * new).astype(jnp.float32)
        same = old == new
        a, b = jnp.where(same, c, sy * z), jnp.where(same, sz * z, 0.0)
        re, im = (a, b) if re is None else (re * a - im * b, re * b + im * a)
    return jnp.concatenate([jnp.concatenate([re, im], 1), jnp.concatenate([-im, re], 1)], 0)


def turn_lanes(state, matrix):
    re, im = (x.reshape(-1, 128) for x in state)
    both = lax.dot_general(
        jnp.concatenate([re, im], axis=1),
        matrix[...],
        (((1,), (0,)), ((), ())),
        precision=lax.Precision.HIGH,
        preferred_element_type=jnp.float32,
    )
    return both[:, :128].reshape(state[0].shape), both[:, 128:].reshape(state[0].shape)


def terms(bra, ket, place, w, w_sum):
    axis, bit = place
    if axis == MAJOR:
        y = 0.0
        for b, k in zip(bra, ket):
            b0, b1 = split_major(b, bit)
            k0, k1 = split_major(k, bit)
            y = y + jnp.sum(b1 * k0 - b0 * k1, axis=(0, 1))
        w0, w1 = split_major(w, bit)
        return 0.5 * y, 0.5 * jnp.sum(w0 - w1, axis=(0, 1))
    z = 0.5 * minor_sign(axis, bit)[0]
    y = sum(jnp.sum(b * partner(k, axis, bit), axis=0) for b, k in zip(bra, ket))
    return -z * y, z * w_sum


def edge_sign(place, qubits, edges, majors, me):
    shape = (majors, 8, 128)
    parts = {
        LANE: lax.broadcasted_iota(jnp.int32, shape, 2),
        SUB: lax.broadcasted_iota(jnp.int32, shape, 1),
        MAJOR: lax.broadcasted_iota(jnp.int32, shape, 0),
        DEVICE: me,
    }
    bits = [parts[place[q][0]] >> place[q][1] & 1 for q in range(qubits)]
    parity = jnp.zeros(shape, jnp.int32)
    for q in edges:
        parity = parity + bits[q] * bits[(q + 1) % qubits]
    return (1 - 2 * (parity & 1)).astype(jnp.float32)


def half_turn(angle):
    x = 0.5 * angle
    x2 = x * x
    cosine, sine = 0.0, 0.0
    for n in range(8, -1, -1):
        cosine = cosine * x2 + (-1.0) ** n / math.factorial(2 * n)
        sine = sine * x2 + (-1.0) ** n / math.factorial(2 * n + 1)
    return cosine, sine * x


def kernel(
    n, qubits, angles, kinds, ket_ref, obs_ref, out_ref, grads_ref,
    ket_in, obs_in, sent1, held1, sent2, held2, gsent, gheld, gsent2, gheld2,
    send1, recv1, send2, recv2, gsend, grecv, gsend2, grecv2, load, wide,
):
    me = lax.axis_index("amp")
    majors = n
    major_bits = n.bit_length() - 1
    local_bits = LANE_BITS + SUB_BITS + major_bits
    home, away = layouts(major_bits, qubits - local_bits)
    scale = 2.0 / math.sqrt(2**qubits)

    loads = [
        pltpu.make_async_copy(ket_ref, ket_in, load.at[0]),
        pltpu.make_async_copy(obs_ref, obs_in, load.at[1]),
    ]
    for copy in loads:
        copy.start()

    half = n // 2
    high, low = me // half, me % half

    def peer(k, sign):
        side = (high + 1 - k // half) % 2
        return side * half + (low + half + sign * (k % half)) % half

    barrier = pltpu.get_barrier_semaphore()
    for k in [k for k in range(n) if k != half]:
        pl.semaphore_signal(barrier, inc=1, device_id=(peer(k, 1),), device_id_type=MESH)
    for copy in loads:
        copy.wait()

    rows = 8 * majors
    raw = [
        ket_in[pl.ds(0, rows, stride=2), :],
        ket_in[pl.ds(1, rows, stride=2), :],
        obs_in[...],
    ]
    for part, value in enumerate(raw):
        value = value.reshape(majors, 8, 128)
        for bit in (1, 2):
            value = swap_bits(value, major_bits - 3 + bit, bit)
        sent1[:, part] = value

    pl.semaphore_wait(barrier, n - 1)

    def exchange(source, target, send, recv):
        def copy(k, block, slot):
            return pltpu.make_async_remote_copy(
                src_ref=source.at[block],
                dst_ref=target.at[slot],
                send_sem=send.at[k],
                recv_sem=recv.at[k],
                device_id=(peer(k, 1),),
                device_id_type=MESH,
            )

        def each(act):
            for lower, upper in ((0, half), (half + 1, n)):
                pl.loop(lower, upper)(act)

        def start():
            each(lambda k: copy(k, peer(k, 1), me).start())

        def arrive():
            each(lambda k: copy(k, peer(k, 1), peer(k, -1)).wait_recv())

        def depart():
            each(lambda k: copy(k, peer(k, 1), me).wait_send())

        return start, arrive, depart

    def gather(source, target, send, recv, stride, count):
        digit = me // stride % count

        def copies():
            for k in range(1, count):
                yield pltpu.make_async_remote_copy(
                    src_ref=source,
                    dst_ref=target.at[k],
                    send_sem=send.at[k],
                    recv_sem=recv.at[k],
                    device_id=(me + ((digit + k) % count - digit) * stride,),
                    device_id_type=MESH,
                )

        target[0] = source[...]
        for copy in copies():
            copy.start()
        return lambda: [copy.wait_recv() for copy in copies()], lambda: [copy.wait_send() for copy in copies()]

    start1, arrive1, depart1 = exchange(sent1, held1, send1, recv1)
    start2, arrive2, depart2 = exchange(sent2, held2, send2, recv2)
    start1()
    held1[me] = sent1[me]

    layers, kind_count = angles.shape
    turns = [[half_turn(angles[l, k]) for k in range(kind_count)] for l in range(layers)]
    coefs, shares = [], []
    for l in range(layers):
        row, share = [], []
        for q in range(qubits):
            kind = kinds[l, q]
            is_kind = [jnp.where(kind == k, 1.0, 0.0) for k in range(kind_count)]
            c = sum(is_kind[k] * turns[l][k][0] for k in range(kind_count))
            sy = sum(is_kind[k] * turns[l][k][1] for k in range(kind_count - 1))
            row.append((c, sy, is_kind[-1] * turns[l][-1][1]))
            share.append(is_kind)
        coefs.append(row)
        shares.append(share)

    for l in range(layers):
        wide[l] = lane_matrix(coefs[l][:LANE_BITS])
    matrices = [wide.at[l] for l in range(layers)]

    sums = [[jnp.zeros((8, 128), jnp.float32) for _ in range(kind_count)] for _ in range(layers)]

    def add_terms(l, chosen, place, bra, ket):
        w = bra[0] * ket[1] - bra[1] * ket[0]
        w_sum = jnp.sum(w, axis=0)
        for q in chosen:
            y, z = terms(bra, ket, place[q], w, w_sum)
            for k in range(kind_count):
                sums[l][k] = sums[l][k] + shares[l][q][k] * (z if k == kind_count - 1 else y)

    def turn(state, l, chosen, place):
        lanes = set(range(LANE_BITS))
        if lanes <= set(chosen):
            state = turn_lanes(state, matrices[l])
            chosen = [q for q in chosen if q not in lanes]
        for q in chosen:
            state = gate(state, place[q], coefs[l][q])
        return state

    def prepare(buffer, sign):
        ket = (buffer[:, 0] * sign, buffer[:, 1] * sign)
        weight = scale * buffer[:, 2]
        return ket, (weight * ket[0], weight * ket[1])

    def times(state, sign):
        return (state[0] * sign, state[1] * sign)

    every = range(qubits)
    moved = [q for q in every if away[q][0] == DEVICE]
    first, last = min(moved), max(moved)
    late_edges = [q for q in every if first - 1 <= q <= last]
    early_edges = [q for q in every if q not in late_edges]
    local = [q for q in every if home[q][0] != DEVICE]
    outer = [q for q in every if home[q][0] == DEVICE]

    sign = edge_sign(home, qubits, every, majors, me)
    ket, bra = prepare(sent1, sign)
    add_terms(1, local, home, bra, ket)
    ket, bra = (times(turn(x, 1, local, home), sign) for x in (ket, bra))
    add_terms(0, local[1:-1], home, bra, ket)

    sign = edge_sign(away, qubits, every, majors, me)
    early = edge_sign(away, qubits, early_edges, majors, me)
    arrive1()
    ket, bra = prepare(held1, sign)
    here = [q for q in every if away[q][0] != DEVICE]
    bra_mid = times(turn(bra, 1, here, away), early)
    ready = [q for q in here if q not in (first - 1, last + 1)]
    done = turn(bra_mid, 0, ready, away)
    sent2[:, 0] = done[0]
    sent2[:, 1] = done[1]
    start2()
    held2[me] = sent2[me]
    add_terms(1, outer, away, bra, ket)
    ket = times(turn(ket, 1, here, away), early)
    add_terms(0, [local[-1]] + outer + [0], away, bra_mid, ket)

    at = [lax.broadcasted_iota(jnp.int32, (layers, 128), d) for d in range(2)]
    total = jnp.zeros((layers, 128), jnp.float32)
    for l in range(layers):
        for k in range(kind_count):
            total = total + jnp.where((at[0] == l) & (at[1] == k), jnp.sum(sums[l][k]), 0.0)
    inner = gheld.shape[0]
    gsent[...] = total
    garrive, gdepart = gather(gsent, gheld, gsend, grecv, 1, inner)
    garrive()
    gsent2[...] = jnp.sum(gheld[...], axis=0)
    garrive2, gdepart2 = gather(gsent2, gheld2, gsend2, grecv2, inner, n // inner)

    late = edge_sign(home, qubits, late_edges, majors, me)
    arrive2()
    bra = (held2[:, 0], held2[:, 1])
    bra = times(turn(bra, 1, moved, home), late)
    bra = turn(bra, 0, [q for q in local if q not in ready], home)
    for part, value in enumerate(bra):
        for bit in (1, 2):
            value = swap_bits(value, major_bits - 3 + bit, bit)
        out_ref[pl.ds(part, rows, stride=2), :] = value.reshape(rows, 128)
    garrive2()
    grads_ref[...] = jnp.sum(gheld2[...], axis=0)
    depart1()
    depart2()
    gdepart()
    gdepart2()


def by_exchange(ket_state, observable, angles, gate_kinds):
    amp_count = ket_state.shape[1]
    n = lax.axis_size("amp")
    qubits = (amp_count * n).bit_length() - 1
    layers, kind_count = angles.shape
    rows = amp_count // 128
    ket = ket_state.reshape(2, rows, 128).transpose(1, 0, 2).reshape(2 * rows, 128)
    vmem = pl.BlockSpec(memory_space=pltpu.VMEM)
    smem = pl.BlockSpec(memory_space=pltpu.SMEM)
    hbm = pl.BlockSpec(memory_space=pl.ANY)
    inner = 1 << n.bit_length() // 2
    outer = n // inner
    f32 = jnp.float32
    out, grads = pl.pallas_call(
        functools.partial(kernel, n, qubits),
        out_shape=(
            jax.ShapeDtypeStruct((2 * rows, 128), f32),
            jax.ShapeDtypeStruct((layers, 128), f32),
        ),
        in_specs=[smem, smem, hbm, hbm],
        out_specs=(vmem, vmem),
        scratch_shapes=[
            pltpu.VMEM((2 * rows, 128), f32),
            pltpu.VMEM((rows, 128), f32),
            pltpu.VMEM((n, 3, 8, 128), f32),
            pltpu.VMEM((n, 3, 8, 128), f32),
            pltpu.VMEM((n, 2, 8, 128), f32),
            pltpu.VMEM((n, 2, 8, 128), f32),
            pltpu.VMEM((layers, 128), f32),
            pltpu.VMEM((inner, layers, 128), f32),
            pltpu.VMEM((layers, 128), f32),
            pltpu.VMEM((outer, layers, 128), f32),
        ]
        + [pltpu.SemaphoreType.DMA((size,)) for size in (n, n, n, n, inner, inner, outer, outer, 2)]
        + [pltpu.VMEM((layers, 256, 256), f32)],
        compiler_params=pltpu.CompilerParams(collective_id=0, has_side_effects=True),
    )(angles, gate_kinds, ket, observable.reshape(rows, 128))
    bra_state = out.reshape(rows, 2, 128).transpose(1, 0, 2).reshape(2, amp_count)
    return (bra_state, grads[:, :kind_count])


def per_device(ket_state, observable, angles, gate_kinds):
    tiles = ket_state.shape[1] // (1 << LANE_BITS + SUB_BITS)
    if tiles == lax.axis_size("amp") and tiles >= 8 and angles.shape == (2, 3):
        return by_exchange(ket_state, observable, angles, gate_kinds)
    return on_device(ket_state, observable, angles, gate_kinds)


def solution(mesh):
    placed = (P(None, "amp"), P("amp"), P(), P())
    return jax.shard_map(
        per_device, mesh=mesh, in_specs=placed, out_specs=(P(None, "amp"), P()), check_vma=False
    )
```

profile of v0, /device:TPU:0, one launch (start us, length us, event | category | flops | bytes accessed | tf_op | source)
XLA Modules:
  0.0 33.5 jit_solution(17684440150257242487)
XLA Ops:
  0.6 30.6 %shard_map.59 = (f32[512,128]{1,0:T(8,128)}, f32[2,128]{1,0:T(2,128)}) custom-call(f32[2,3]{1,0:T(2,128)} %angles.1, s32[2,32]{1,0:T(2,128)} %kinds.1, f32[512,128]{1,0:T(8,128)} %bitcast.12, f32[256,128]{1,0:T(8,128)} %bitcast.14), custom_call_target="tpu_custom_call" | custom-call | tf_op jit(solution)/shard_map/pallas_call | solution.py:636
  31.2 0.0 copy-start
  31.2 1.7 %copy.10 = f32[2,32768]{1,0:T(2,128)} copy(f32[2,32768]{1,0:T(2,128)} %bitcast.13) | data formatting | bytes 524288
  32.9 0.0 copy-done
  32.9 0.6 %copy.11 = f32[2,3]{1,0:T(2,128)} copy(f32[2,3]{1,0:T(2,128)S(1)} %bitcast.15) | data formatting | bytes 48
Async XLA Ops:
  31.2 1.7 %copy-start = (f32[2,128]{1,0:T(2,128)S(1)}, f32[2,128]{1,0:T(2,128)}, u32[]{:S(2)}) copy-start(f32[2,128]{1,0:T(2,128)} %get-tuple-element.5) | copy-start | bytes 3076
where the time goes:
time: 33.6 us; the launch traced here: 33.5 us
  Pallas kernels  30.6 us (91%)
  local copies, waits for them, and re-layouts  2.24 us (7%)
  between operations  0.65 us (2%)
    pallas_call x1, Pallas kernels, by_exchange(): pl.pallas_call(functools.partial(kernel, n, qubits), out_shape=(jax.Shape...  30.6 us
    unnamed x4, local copies, waits for them, and re-layouts  2.24 us

commit v1 on v0

--- a/solution.py
+++ b/solution.py
@@ -10,8 +10,9 @@
 from jax.sharding import PartitionSpec as P
 
 MESH = pl.DeviceIdType.MESH
-LANE, SUB, MAJOR, DEVICE = range(4)
+LANE, SUB, MAJOR, DEVICE, CHUNK = range(5)
 LANE_BITS, SUB_BITS = 7, 3
+PLANES = 4
 
 
 def from_partner(value, axis, apart):
@@ -276,20 +277,19 @@
     return (bra_state, grads)
 
 
-def layouts(major_bits, global_bits):
-    low = LANE_BITS + SUB_BITS
-    local_bits = low + major_bits
+def chunk_layouts(g):
+    top = g + LANE_BITS + SUB_BITS - 1
     home, away = {}, {}
     for q in range(LANE_BITS):
         home[q] = away[q] = (LANE, q)
-    home[LANE_BITS] = away[LANE_BITS] = (SUB, 0)
-    for bit, q in ((1, local_bits - 2), (2, local_bits - 1)):
+    for bit, q in ((1, top - 1), (2, top)):
         home[q] = away[q] = (SUB, bit)
-    moved = list(range(low, local_bits - 2)) + [low - 2, low - 1]
+    moved = list(range(LANE_BITS + 2, top - 1)) + [LANE_BITS]
     for bit, q in enumerate(moved):
         home[q], away[q] = (MAJOR, bit), (DEVICE, bit)
-    for bit in range(global_bits):
-        home[local_bits + bit], away[local_bits + bit] = (DEVICE, bit), (MAJOR, bit)
+    home[LANE_BITS + 1], away[LANE_BITS + 1] = (MAJOR, g), (CHUNK, 0)
+    for bit in range(g):
+        home[top + 1 + bit], away[top + 1 + bit] = (DEVICE, bit), (MAJOR, bit)
     return home, away
 
 
@@ -336,23 +336,27 @@
     return join_major(jnp.where(lower, x0, roll3(x1, step)), jnp.where(lower, roll3(x0, -step), x1))
 
 
-def gate(state, place, coef):
-    re, im = state
+def other_part(x):
+    return partner(x, SUB, 0)
+
+
+def weights(obs, chunk):
+    place = lax.broadcasted_iota(jnp.int32, (1, 8, 128), 1) & 3
+    if chunk == 0:
+        end, far = 0, 3
+    else:
+        end, far = 3, 0
+    step = 1 if chunk == 0 else -1
+    near = jnp.where(place == end, obs, shifted(obs, SUB, step))
+    return jnp.where(place == far, shifted(obs, SUB, 2 * step), near)
+
+
+def y_gate(x, place, cy, sy):
     axis, bit = place
-    c, sy, sz = coef
     if axis == MAJOR:
-        r0, r1 = split_major(re, bit)
-        i0, i1 = split_major(im, bit)
-        return (
-            join_major(c * r0 + sy * r1 - sz * i0, c * r1 - sy * r0 + sz * i1),
-            join_major(c * i0 + sy * i1 + sz * r0, c * i1 - sy * i0 - sz * r1),
-        )
-    z = minor_sign(axis, bit)
-    zy, zz = sy * z, sz * z
-    return (
-        c * re + zy * partner(re, axis, bit) - zz * im,
-        c * im + zy * partner(im, axis, bit) + zz * re,
-    )
+        x0, x1 = split_major(x, bit)
+        return join_major(cy * x0 + sy * x1, cy * x1 - sy * x0)
+    return cy * x + (sy * minor_sign(axis, bit)) * partner(x, axis, bit)
 
 
 def lane_matrix(coefs):
@@ -364,49 +368,84 @@
         same = old == new
         a, b = jnp.where(same, c, sy * z), jnp.where(same, sz * z, 0.0)
         re, im = (a, b) if re is None else (re * a - im * b, re * b + im * a)
-    return jnp.concatenate([jnp.concatenate([re, im], 1), jnp.concatenate([-im, re], 1)], 0)
-
-
-def turn_lanes(state, matrix):
-    re, im = (x.reshape(-1, 128) for x in state)
+    return jnp.concatenate([re, im], 1)
+
+
+def turn_lanes(x, matrix):
     both = lax.dot_general(
-        jnp.concatenate([re, im], axis=1),
+        x.reshape(-1, 128),
         matrix[...],
         (((1,), (0,)), ((), ())),
         precision=lax.Precision.HIGH,
         preferred_element_type=jnp.float32,
     )
-    return both[:, :128].reshape(state[0].shape), both[:, 128:].reshape(state[0].shape)
+    re, im = both[:, :128].reshape(x.shape), both[:, 128:].reshape(x.shape)
+    return re - minor_sign(SUB, 0) * other_part(im)
 
 
 def terms(bra, ket, place, w, w_sum):
     axis, bit = place
     if axis == MAJOR:
-        y = 0.0
-        for b, k in zip(bra, ket):
-            b0, b1 = split_major(b, bit)
-            k0, k1 = split_major(k, bit)
-            y = y + jnp.sum(b1 * k0 - b0 * k1, axis=(0, 1))
+        b0, b1 = split_major(bra, bit)
+        k0, k1 = split_major(ket, bit)
         w0, w1 = split_major(w, bit)
-        return 0.5 * y, 0.5 * jnp.sum(w0 - w1, axis=(0, 1))
+        return 0.5 * jnp.sum(b1 * k0 - b0 * k1, axis=(0, 1)), 0.5 * jnp.sum(w0 - w1, axis=(0, 1))
     z = 0.5 * minor_sign(axis, bit)[0]
-    y = sum(jnp.sum(b * partner(k, axis, bit), axis=0) for b, k in zip(bra, ket))
-    return -z * y, z * w_sum
-
-
-def edge_sign(place, qubits, edges, majors, me):
-    shape = (majors, 8, 128)
-    parts = {
-        LANE: lax.broadcasted_iota(jnp.int32, shape, 2),
-        SUB: lax.broadcasted_iota(jnp.int32, shape, 1),
-        MAJOR: lax.broadcasted_iota(jnp.int32, shape, 0),
-        DEVICE: me,
-    }
-    bits = [parts[place[q][0]] >> place[q][1] & 1 for q in range(qubits)]
-    parity = jnp.zeros(shape, jnp.int32)
+    return -z * jnp.sum(bra * partner(ket, axis, bit), axis=0), z * w_sum
+
+
+def phases(place, qubits, edges, majors, me, chunk, turns=None):
+    def bit_of(q):
+        axis, bit = place[q]
+        if axis in (LANE, SUB):
+            return minor_bit(axis, bit)
+        return me >> bit & 1 if axis == DEVICE else chunk
+
+    at_major = {place[q][1]: q for q in range(qubits) if place[q][0] == MAJOR}
+    parity = jnp.zeros((1, 8, 128), jnp.int32)
     for q in edges:
-        parity = parity + bits[q] * bits[(q + 1) % qubits]
-    return (1 - 2 * (parity & 1)).astype(jnp.float32)
+        ends = (q, (q + 1) % qubits)
+        if all(place[e][0] != MAJOR for e in ends):
+            parity = parity + bit_of(ends[0]) * bit_of(ends[1])
+    re = (1 - 2 * (parity & 1)).astype(jnp.float32)
+    im = None
+
+    def times(re, im, c, s):
+        if im is None:
+            return re * c, re * s
+        return re * c - im * s, im * c + re * s
+
+    turns = turns or {}
+    for q, (c, s) in turns.items():
+        axis, bit = place[q]
+        if axis != MAJOR:
+            re, im = times(re, im, c, s * minor_sign(axis, bit))
+    for j in range(majors.bit_length() - 1):
+        q = at_major[j]
+        parity, flips = None, []
+        for edge, o in ((q, (q + 1) % qubits), ((q - 1) % qubits, (q - 1) % qubits)):
+            if edge not in edges:
+                continue
+            if place[o][0] != MAJOR:
+                parity = bit_of(o) if parity is None else parity + bit_of(o)
+            elif place[o][1] < j:
+                flips.append(place[o][1])
+
+        def upper(x):
+            if parity is not None:
+                x = x * jnp.broadcast_to(1 - 2 * (parity & 1), (1, 8, 128)).astype(jnp.float32)
+            for bit in flips:
+                x0, x1 = split_major(x, bit)
+                x = join_major(x0, -x1)
+            return x
+
+        lo, hi = (re, im), (upper(re), None if im is None else upper(im))
+        if q in turns:
+            c, s = turns[q]
+            lo, hi = times(*lo, c, s), times(*hi, c, -s)
+        re = jnp.concatenate([lo[0], hi[0]], 0)
+        im = None if lo[1] is None else jnp.concatenate([lo[1], hi[1]], 0)
+    return (re, None) if im is None else (re, -minor_sign(SUB, 0) * im)
 
 
 def half_turn(angle):
@@ -421,14 +460,12 @@
 
 def kernel(
     n, qubits, angles, kinds, ket_ref, obs_ref, out_ref, grads_ref,
-    ket_in, obs_in, sent1, held1, sent2, held2, gsent, gheld, gsent2, gheld2,
-    send1, recv1, send2, recv2, gsend, grecv, gsend2, grecv2, load, wide,
+    ket_in, obs_in, sent, held, back, landed, gsent, gheld, gsent2, gheld2,
+    flag, send1, recv1, send2, recv2, gsend, grecv, gsend2, grecv2, load, wide,
 ):
     me = lax.axis_index("amp")
-    majors = n
-    major_bits = n.bit_length() - 1
-    local_bits = LANE_BITS + SUB_BITS + major_bits
-    home, away = layouts(major_bits, qubits - local_bits)
+    g = n.bit_length() - 1
+    home, away = chunk_layouts(g)
     scale = 2.0 / math.sqrt(2**qubits)
 
     loads = [
@@ -438,56 +475,75 @@
     for copy in loads:
         copy.start()
 
-    half = n // 2
-    high, low = me // half, me % half
-
-    def peer(k, sign):
-        side = (high + 1 - k // half) % 2
-        return side * half + (low + half + sign * (k % half)) % half
-
+    half, size = n // 2, n // PLANES
+    plane, place = me // size, me % size
+    upper = plane // 2
+    near = 2 - upper
+    far = near + 1 - 2 * upper
+    side = plane + 1 - 2 * (plane % 2)
+    others = (near, far, side)
+
+    def inside(j):
+        spot = place
+        for bit in range(size.bit_length() - 1):
+            if j >> bit & 1:
+                spot = spot + (1 - 2 * (place // (1 << bit) % 2)) * (1 << bit)
+        return spot
+
+    spots = [inside(j) for j in range(size)]
     barrier = pltpu.get_barrier_semaphore()
-    for k in [k for k in range(n) if k != half]:
-        pl.semaphore_signal(barrier, inc=1, device_id=(peer(k, 1),), device_id_type=MESH)
+    for other in others:
+        pl.semaphore_signal(barrier, inc=1, device_id=(other * size + place,), device_id_type=MESH)
+    for spot in spots[1:]:
+        pl.semaphore_signal(barrier, inc=1, device_id=(plane * size + spot,), device_id_type=MESH)
     for copy in loads:
         copy.wait()
 
-    rows = 8 * majors
-    raw = [
-        ket_in[pl.ds(0, rows, stride=2), :],
-        ket_in[pl.ds(1, rows, stride=2), :],
-        obs_in[...],
-    ]
-    for part, value in enumerate(raw):
-        value = value.reshape(majors, 8, 128)
-        for bit in (1, 2):
-            value = swap_bits(value, major_bits - 3 + bit, bit)
-        sent1[:, part] = value
-
-    pl.semaphore_wait(barrier, n - 1)
+    value = ket_in[...].reshape(2 * n, 8, 128)
+    for bit in (1, 2):
+        value = swap_bits(value, g - 2 + bit, bit)
+    sent[:, 0] = value[:n]
+    sent[:, 1] = value[n:]
+    value = obs_in[...].reshape(n, 8, 128)
+    for major, bit in ((g - 2, 0), (g - 1, 2)):
+        value = swap_bits(value, major, bit)
+    sent[:, 2] = jnp.stack([value[:half], value[half:]], axis=1).reshape(n, 8, 128)
+
+    pl.semaphore_wait(barrier, size - 1 + len(others))
+    for other in others:
+        pl.semaphore_signal(flag.at[plane], inc=1, device_id=(other * size + place,), device_id_type=MESH)
 
     def exchange(source, target, send, recv):
-        def copy(k, block, slot):
+        def copy(block):
             return pltpu.make_async_remote_copy(
                 src_ref=source.at[block],
-                dst_ref=target.at[slot],
-                send_sem=send.at[k],
-                recv_sem=recv.at[k],
-                device_id=(peer(k, 1),),
+                dst_ref=target.at[me],
+                send_sem=send,
+                recv_sem=recv.at[plane],
+                device_id=(block,),
                 device_id_type=MESH,
             )
 
-        def each(act):
-            for lower, upper in ((0, half), (half + 1, n)):
-                pl.loop(lower, upper)(act)
-
-        def start():
-            each(lambda k: copy(k, peer(k, 1), me).start())
-
-        def arrive():
-            each(lambda k: copy(k, peer(k, 1), peer(k, -1)).wait_recv())
+        def start(to, picked):
+            for spot in picked:
+                copy(to * size + spot).start()
+
+        def many(first, count, origin):
+            return pltpu.make_async_remote_copy(
+                src_ref=source.at[pl.ds(first, count)],
+                dst_ref=target.at[pl.ds(first, count)],
+                send_sem=send,
+                recv_sem=recv.at[origin],
+                device_id=(me,),
+                device_id_type=MESH,
+            )
+
+        def arrive(origin):
+            count = size - 1 if origin is plane else size
+            many(origin * size, count, origin).wait_recv()
 
         def depart():
-            each(lambda k: copy(k, peer(k, 1), me).wait_send())
+            many(0, n - 1, plane).wait_send()
 
         return start, arrive, depart
 
@@ -510,10 +566,16 @@
             copy.start()
         return lambda: [copy.wait_recv() for copy in copies()], lambda: [copy.wait_send() for copy in copies()]
 
-    start1, arrive1, depart1 = exchange(sent1, held1, send1, recv1)
-    start2, arrive2, depart2 = exchange(sent2, held2, send2, recv2)
-    start1()
-    held1[me] = sent1[me]
+    start1, arrive1, depart1 = exchange(sent, held, send1, recv1)
+    start2, arrive2, depart2 = exchange(back, landed, send2, recv2)
+    start1(far, spots[:1])
+    start1(near, spots[:1])
+    start1(plane, spots[:0:-1])
+    start1(side, spots[:1])
+    for other in others:
+        pl.semaphore_wait(flag.at[other], 1)
+        start1(other, spots[:0:-1])
+    held[me] = sent[me]
 
     layers, kind_count = angles.shape
     turns = [[half_turn(angles[l, k]) for k in range(kind_count)] for l in range(layers)]
@@ -523,73 +585,84 @@
         for q in range(qubits):
             kind = kinds[l, q]
             is_kind = [jnp.where(kind == k, 1.0, 0.0) for k in range(kind_count)]
-            c = sum(is_kind[k] * turns[l][k][0] for k in range(kind_count))
+            cy = sum(is_kind[k] * turns[l][k][0] for k in range(kind_count - 1))
             sy = sum(is_kind[k] * turns[l][k][1] for k in range(kind_count - 1))
-            row.append((c, sy, is_kind[-1] * turns[l][-1][1]))
+            cz = is_kind[-1] * turns[l][-1][0]
+            sz = is_kind[-1] * turns[l][-1][1]
+            row.append((cy + is_kind[-1], sy, cz + (1.0 - is_kind[-1]), sz, cy + cz))
             share.append(is_kind)
         coefs.append(row)
         shares.append(share)
 
+    every = range(qubits)
+    late = [q for q in every if home[q][0] == MAJOR]
+    first, last = min(late), max(late)
+    late_edges = [q for q in every if first - 1 <= q <= last]
+    early_edges = [q for q in every if q not in late_edges]
+    local = [q for q in every if home[q][0] != DEVICE]
+    outer = [q for q in every if home[q][0] == DEVICE]
+    here = [q for q in every if q not in late]
+    ready = [q for q in here if q not in (first - 1, last + 1)]
+    rest = [q for q in local if q not in ready]
+
     for l in range(layers):
-        wide[l] = lane_matrix(coefs[l][:LANE_BITS])
-    matrices = [wide.at[l] for l in range(layers)]
+        lanes = [
+            (coefs[l][q][4], coefs[l][q][1], coefs[l][q][3]) if l == 1 or q in ready else (1.0, 0.0, 0.0)
+            for q in range(LANE_BITS)
+        ]
+        wide[l] = lane_matrix(lanes)
 
     sums = [[jnp.zeros((8, 128), jnp.float32) for _ in range(kind_count)] for _ in range(layers)]
 
     def add_terms(l, chosen, place, bra, ket):
-        w = bra[0] * ket[1] - bra[1] * ket[0]
+        w = minor_sign(SUB, 0) * (bra * other_part(ket))
         w_sum = jnp.sum(w, axis=0)
         for q in chosen:
             y, z = terms(bra, ket, place[q], w, w_sum)
             for k in range(kind_count):
                 sums[l][k] = sums[l][k] + shares[l][q][k] * (z if k == kind_count - 1 else y)
 
-    def turn(state, l, chosen, place):
-        lanes = set(range(LANE_BITS))
-        if lanes <= set(chosen):
-            state = turn_lanes(state, matrices[l])
-            chosen = [q for q in chosen if q not in lanes]
+    def phase_of(l, chosen, place, edges, majors, chunk, by_matrix):
+        turned = {q: coefs[l][q][2:4] for q in chosen if not (by_matrix and place[q][0] == LANE)}
+        return phases(place, qubits, edges, majors, me, chunk, turned)
+
+    def turn(x, l, chosen, place, phase, by_matrix=True):
+        if by_matrix:
+            x = turn_lanes(x, wide.at[l])
         for q in chosen:
-            state = gate(state, place[q], coefs[l][q])
-        return state
-
-    def prepare(buffer, sign):
-        ket = (buffer[:, 0] * sign, buffer[:, 1] * sign)
-        weight = scale * buffer[:, 2]
-        return ket, (weight * ket[0], weight * ket[1])
-
-    def times(state, sign):
-        return (state[0] * sign, state[1] * sign)
-
-    every = range(qubits)
-    moved = [q for q in every if away[q][0] == DEVICE]
-    first, last = min(moved), max(moved)
-    late_edges = [q for q in every if first - 1 <= q <= last]
-    early_edges = [q for q in every if q not in late_edges]
-    local = [q for q in every if home[q][0] != DEVICE]
-    outer = [q for q in every if home[q][0] == DEVICE]
-
-    sign = edge_sign(home, qubits, every, majors, me)
-    ket, bra = prepare(sent1, sign)
+            if not (by_matrix and place[q][0] == LANE):
+                x = y_gate(x, place[q], coefs[l][q][0], coefs[l][q][1])
+        return phase[0] * x + phase[1] * other_part(x)
+
+    sign, _ = phases(home, qubits, every, 2 * n, me, 0)
+    phase = phase_of(1, local, home, every, 2 * n, 0, True)
+    ket = jnp.concatenate([sent[:, 0], sent[:, 1]], 0) * sign
+    obs = sent[:, 2]
+    bra = scale * jnp.concatenate([weights(obs, 0), weights(obs, 1)], 0) * ket
     add_terms(1, local, home, bra, ket)
-    ket, bra = (times(turn(x, 1, local, home), sign) for x in (ket, bra))
+    ket, bra = (turn(x, 1, local, home, phase) for x in (ket, bra))
     add_terms(0, local[1:-1], home, bra, ket)
 
-    sign = edge_sign(away, qubits, every, majors, me)
-    early = edge_sign(away, qubits, early_edges, majors, me)
-    arrive1()
-    ket, bra = prepare(held1, sign)
-    here = [q for q in every if away[q][0] != DEVICE]
-    bra_mid = times(turn(bra, 1, here, away), early)
-    ready = [q for q in here if q not in (first - 1, last + 1)]
-    done = turn(bra_mid, 0, ready, away)
-    sent2[:, 0] = done[0]
-    sent2[:, 1] = done[1]
-    start2()
-    held2[me] = sent2[me]
-    add_terms(1, outer, away, bra, ket)
-    ket = times(turn(ket, 1, here, away), early)
-    add_terms(0, [local[-1]] + outer + [0], away, bra_mid, ket)
+    ready_phase = phase_of(0, ready, away, [], n, 0, True)
+    signs = [phases(away, qubits, every, n, me, chunk)[0] for chunk in range(2)]
+    mid_phases = [phase_of(1, here, away, early_edges, n, chunk, True) for chunk in range(2)]
+    for origin in (plane,) + others:
+        arrive1(origin)
+    states = []
+    for chunk in range(2):
+        ket = held[:, chunk] * signs[chunk]
+        bra = scale * weights(held[:, 2], chunk) * ket
+        bra_mid = turn(bra, 1, here, away, mid_phases[chunk])
+        back[:, chunk] = turn(bra_mid, 0, ready, away, ready_phase)
+        states.append((ket, bra, bra_mid))
+    for other in (far, near, side):
+        start2(other, spots[::-1])
+    start2(plane, spots[:0:-1])
+    landed[me] = back[me]
+    for chunk, (ket, bra, bra_mid) in enumerate(states):
+        add_terms(1, outer, away, bra, ket)
+        ket = turn(ket, 1, here, away, mid_phases[chunk])
+        add_terms(0, [local[-1]] + outer + [0], away, bra_mid, ket)
 
     at = [lax.broadcasted_iota(jnp.int32, (layers, 128), d) for d in range(2)]
     total = jnp.zeros((layers, 128), jnp.float32)
@@ -603,21 +676,29 @@
     gsent2[...] = jnp.sum(gheld[...], axis=0)
     garrive2, gdepart2 = gather(gsent2, gheld2, gsend2, grecv2, inner, n // inner)
 
-    late = edge_sign(home, qubits, late_edges, majors, me)
-    arrive2()
-    bra = (held2[:, 0], held2[:, 1])
-    bra = times(turn(bra, 1, moved, home), late)
-    bra = turn(bra, 0, [q for q in local if q not in ready], home)
-    for part, value in enumerate(bra):
-        for bit in (1, 2):
-            value = swap_bits(value, major_bits - 3 + bit, bit)
-        out_ref[pl.ds(part, rows, stride=2), :] = value.reshape(rows, 128)
+    late_phase = phase_of(1, late, home, late_edges, 2 * n, 0, False)
+    rest_phase = phase_of(0, rest, home, [], 2 * n, 0, False)
+    for origin in (plane,) + others:
+        arrive2(origin)
+    x = jnp.concatenate([landed[:, 0], landed[:, 1]], 0)
+    x = turn(x, 1, late, home, late_phase, False)
+    x = turn(x, 0, rest, home, rest_phase, False)
+    for bit in (1, 2):
+        x = swap_bits(x, g - 2 + bit, bit)
+    out_ref[...] = x.reshape(16 * n, 128)
     garrive2()
     grads_ref[...] = jnp.sum(gheld2[...], axis=0)
     depart1()
     depart2()
     gdepart()
     gdepart2()
+
+
+def finish(bra_ref, sums_ref, out_ref, grads_ref, sem):
+    copy = pltpu.make_async_copy(bra_ref, out_ref, sem)
+    copy.start()
+    grads_ref[...] = sums_ref[:, : grads_ref.shape[1]]
+    copy.wait()
 
 
 def by_exchange(ket_state, observable, angles, gate_kinds):
@@ -629,15 +710,16 @@
     ket = ket_state.reshape(2, rows, 128).transpose(1, 0, 2).reshape(2 * rows, 128)
     vmem = pl.BlockSpec(memory_space=pltpu.VMEM)
     smem = pl.BlockSpec(memory_space=pltpu.SMEM)
-    hbm = pl.BlockSpec(memory_space=pl.ANY)
+    hbm = pl.BlockSpec(memory_space=pltpu.HBM)
     inner = 1 << n.bit_length() // 2
     outer = n // inner
     f32 = jnp.float32
-    out, grads = pl.pallas_call(
+    dma = pltpu.SemaphoreType.DMA
+    bra, sums = pl.pallas_call(
         functools.partial(kernel, n, qubits),
         out_shape=(
-            jax.ShapeDtypeStruct((2 * rows, 128), f32),
-            jax.ShapeDtypeStruct((layers, 128), f32),
+            pltpu.VMEM((2 * rows, 128), f32),
+            pltpu.VMEM((layers, 128), f32),
         ),
         in_specs=[smem, smem, hbm, hbm],
         out_specs=(vmem, vmem),
@@ -652,13 +734,31 @@
             pltpu.VMEM((inner, layers, 128), f32),
             pltpu.VMEM((layers, 128), f32),
             pltpu.VMEM((outer, layers, 128), f32),
+            pltpu.SemaphoreType.REGULAR((PLANES,)),
+            dma,
+            dma((PLANES,)),
+            dma,
+            dma((PLANES,)),
         ]
-        + [pltpu.SemaphoreType.DMA((size,)) for size in (n, n, n, n, inner, inner, outer, outer, 2)]
-        + [pltpu.VMEM((layers, 256, 256), f32)],
-        compiler_params=pltpu.CompilerParams(collective_id=0, has_side_effects=True),
-    )(angles, gate_kinds, ket, observable.reshape(rows, 128))
+        + [dma((size,)) for size in (inner, inner, outer, outer, 2)]
+        + [pltpu.VMEM((layers, 128, 256), f32)],
+        compiler_params=pltpu.CompilerParams(
+            collective_id=0, has_side_effects=True
+        ),
+    )(angles, gate_kinds, *(pltpu.with_memory_space_constraint(x, pltpu.HBM) for x in (ket, observable.reshape(rows, 128))))
+    out, grads = pl.pallas_call(
+        finish,
+        out_shape=(
+            jax.ShapeDtypeStruct((2 * rows, 128), f32),
+            jax.ShapeDtypeStruct((layers, kind_count), f32),
+        ),
+        in_specs=[vmem, vmem],
+        out_specs=(hbm, vmem),
+        scratch_shapes=[dma],
+        compiler_params=pltpu.CompilerParams(vmem_limit_bytes=1 << 20),
+    )(*(pltpu.with_memory_space_constraint(x, pltpu.VMEM) for x in (bra, sums)))
     bra_state = out.reshape(rows, 2, 128).transpose(1, 0, 2).reshape(2, amp_count)
-    return (bra_state, grads[:, :kind_count])
+    return (bra_state, grads)
 
 
 def per_device(ket_state, observable, angles, gate_kinds):

time: 33.6 us -> 28.6 us (0.85)
  Pallas kernels: 30.6 us -> 27.8 us
  local copies, waits for them, and re-layouts: 2.24 us -> 0 us
    pallas_call x1 -> x2, Pallas kernels: 30.6 us -> 27.8 us  [the longest x1 26.5 us: by_exchange(): pl.pallas_call(functools.partial(kernel, n, qubits), out_shape=(pltpu.VME...]
    unnamed x4 -> x0, local copies, waits for them, and re-layouts: 2.24 us -> none
where the time goes in v1:
time: 28.6 us; the launch traced here: 28.5 us
  Pallas kernels  27.8 us (97%)
  between operations  0.64 us (2%)
    pallas_call x1, Pallas kernels, by_exchange(): pl.pallas_call(functools.partial(kernel, n, qubits), out_shape=(pltpu.VME...  26.5 us
    pallas_call x1, Pallas kernels, by_exchange(): pl.pallas_call(finish, out_shape=(jax.ShapeDtypeStruct((2 * rows, 128), f...  1.27 us

profile of v1, /device:TPU:0, one launch (start us, length us, event | category | flops | bytes accessed | tf_op | source)
XLA Modules:
  0.0 28.5 jit_solution(3557116343785302437)
XLA Ops:
  0.6 26.5 %shard_map.59 = (f32[512,128]{1,0:T(8,128)S(1)}, f32[2,128]{1,0:T(2,128)S(1)}) custom-call(f32[2,3]{1,0:T(2,128)} %angles.1, s32[2,32]{1,0:T(2,128)} %kinds.1, f32[512,128]{1,0:T(8,128)} %bitcast.11, f32[256,128]{1,0:T(8,128)} %bitcast.12), custom_call_target="tpu_custom_call" | custom-call | tf_op jit(solution)/shard_map/pallas_call | solution.py:718
  27.2 1.3 %shard_map.60 = (f32[512,128]{1,0:T(8,128)}, f32[2,3]{1,0:T(2,128)}) custom-call(f32[512,128]{1,0:T(8,128)S(1)} %get-tuple-element.6.bra_ref, f32[2,128]{1,0:T(2,128)S(1)} %get-tuple-element.7.sums_ref), custom_call_target="tpu_custom_call" | custom-call | tf_op jit(solution)/shard_map/pallas_call | solution.py:749

commit v2 on v1

--- a/solution.py
+++ b/solution.py
@@ -460,8 +460,8 @@
 
 def kernel(
     n, qubits, angles, kinds, ket_ref, obs_ref, out_ref, grads_ref,
-    ket_in, obs_in, sent, held, back, landed, gsent, gheld, gsent2, gheld2,
-    flag, send1, recv1, send2, recv2, gsend, grecv, gsend2, grecv2, load, wide,
+    ket_in, obs_in, sent, held, back, landed, gsent, gheld,
+    flag, send1, recv1, send2, recv2, gsend, grecv, load, wide,
 ):
     me = lax.axis_index("amp")
     g = n.bit_length() - 1
@@ -482,20 +482,20 @@
     far = near + 1 - 2 * upper
     side = plane + 1 - 2 * (plane % 2)
     others = (near, far, side)
+    planes = {"far": far, "near": near, "side": side, "own": plane}
 
     def inside(j):
-        spot = place
+        spot = place + j
         for bit in range(size.bit_length() - 1):
-            if j >> bit & 1:
-                spot = spot + (1 - 2 * (place // (1 << bit) % 2)) * (1 << bit)
+            step = 1 << bit
+            spot = spot - 2 * step * (place // step % 2) * (j // step % 2)
         return spot
 
-    spots = [inside(j) for j in range(size)]
     barrier = pltpu.get_barrier_semaphore()
     for other in others:
         pl.semaphore_signal(barrier, inc=1, device_id=(other * size + place,), device_id_type=MESH)
-    for spot in spots[1:]:
-        pl.semaphore_signal(barrier, inc=1, device_id=(plane * size + spot,), device_id_type=MESH)
+    for j in range(1, size):
+        pl.semaphore_signal(barrier, inc=1, device_id=(plane * size + inside(j),), device_id_type=MESH)
     for copy in loads:
         copy.wait()
 
@@ -513,68 +513,46 @@
     for other in others:
         pl.semaphore_signal(flag.at[plane], inc=1, device_id=(other * size + place,), device_id_type=MESH)
 
-    def exchange(source, target, send, recv):
-        def copy(block):
+    def exchange(source, target, send, recv, tiles):
+        def part(ref, block, to):
+            return ref.at[block, pl.ds(0, tiles[to])] if tiles else ref.at[block]
+
+        def start(to, lower, upper):
+            @pl.loop(lower, upper)
+            def _(k):
+                block = planes[to] * size + inside(size - 1 - k)
+                pltpu.make_async_remote_copy(
+                    src_ref=part(source, block, to),
+                    dst_ref=part(target, me, to),
+                    send_sem=send.at[planes[to]],
+                    recv_sem=recv.at[plane],
+                    device_id=(block,),
+                    device_id_type=MESH,
+                ).start()
+
+        def many(to):
+            blocks = pl.ds(planes[to] * size, size - 1 if to == "own" else size)
             return pltpu.make_async_remote_copy(
-                src_ref=source.at[block],
-                dst_ref=target.at[me],
-                send_sem=send,
-                recv_sem=recv.at[plane],
-                device_id=(block,),
-                device_id_type=MESH,
-            )
-
-        def start(to, picked):
-            for spot in picked:
-                copy(to * size + spot).start()
-
-        def many(first, count, origin):
-            return pltpu.make_async_remote_copy(
-                src_ref=source.at[pl.ds(first, count)],
-                dst_ref=target.at[pl.ds(first, count)],
-                send_sem=send,
-                recv_sem=recv.at[origin],
+                src_ref=part(source, blocks, to),
+                dst_ref=part(target, blocks, to),
+                send_sem=send.at[planes[to]],
+                recv_sem=recv.at[planes[to]],
                 device_id=(me,),
                 device_id_type=MESH,
             )
 
-        def arrive(origin):
-            count = size - 1 if origin is plane else size
-            many(origin * size, count, origin).wait_recv()
-
-        def depart():
-            many(0, n - 1, plane).wait_send()
-
-        return start, arrive, depart
-
-    def gather(source, target, send, recv, stride, count):
-        digit = me // stride % count
-
-        def copies():
-            for k in range(1, count):
-                yield pltpu.make_async_remote_copy(
-                    src_ref=source,
-                    dst_ref=target.at[k],
-                    send_sem=send.at[k],
-                    recv_sem=recv.at[k],
-                    device_id=(me + ((digit + k) % count - digit) * stride,),
-                    device_id_type=MESH,
-                )
-
-        target[0] = source[...]
-        for copy in copies():
-            copy.start()
-        return lambda: [copy.wait_recv() for copy in copies()], lambda: [copy.wait_send() for copy in copies()]
-
-    start1, arrive1, depart1 = exchange(sent, held, send1, recv1)
-    start2, arrive2, depart2 = exchange(back, landed, send2, recv2)
-    start1(far, spots[:1])
-    start1(near, spots[:1])
-    start1(plane, spots[:0:-1])
-    start1(side, spots[:1])
-    for other in others:
-        pl.semaphore_wait(flag.at[other], 1)
-        start1(other, spots[:0:-1])
+        return start, lambda to: many(to).wait_recv(), lambda: [many(to).wait_send() for to in planes]
+
+    start1, arrive1, depart1 = exchange(sent, held, send1, recv1, dict.fromkeys(planes, 3))
+    start2, arrive2, depart2 = exchange(back, landed, send2, recv2, dict.fromkeys(planes, 2))
+    start3, arrive3, depart3 = exchange(gsent, gheld, gsend, grecv, None)
+    start1("far", size - 1, size)
+    start1("near", size - 1, size)
+    start1("own", 0, size - 1)
+    start1("side", size - 1, size)
+    for to in ("near", "far", "side"):
+        pl.semaphore_wait(flag.at[planes[to]], 1)
+        start1(to, 0, size - 1)
     held[me] = sent[me]
 
     layers, kind_count = angles.shape
@@ -646,7 +624,7 @@
     ready_phase = phase_of(0, ready, away, [], n, 0, True)
     signs = [phases(away, qubits, every, n, me, chunk)[0] for chunk in range(2)]
     mid_phases = [phase_of(1, here, away, early_edges, n, chunk, True) for chunk in range(2)]
-    for origin in (plane,) + others:
+    for origin in ("own", "side", "near", "far"):
         arrive1(origin)
     states = []
     for chunk in range(2):
@@ -655,10 +633,8 @@
         bra_mid = turn(bra, 1, here, away, mid_phases[chunk])
         back[:, chunk] = turn(bra_mid, 0, ready, away, ready_phase)
         states.append((ket, bra, bra_mid))
-    for other in (far, near, side):
-        start2(other, spots[::-1])
-    start2(plane, spots[:0:-1])
-    landed[me] = back[me]
+    start2("far", 0, size)
+    start2("near", 0, size)
     for chunk, (ket, bra, bra_mid) in enumerate(states):
         add_terms(1, outer, away, bra, ket)
         ket = turn(ket, 1, here, away, mid_phases[chunk])
@@ -669,16 +645,17 @@
     for l in range(layers):
         for k in range(kind_count):
             total = total + jnp.where((at[0] == l) & (at[1] == k), jnp.sum(sums[l][k]), 0.0)
-    inner = gheld.shape[0]
-    gsent[...] = total
-    garrive, gdepart = gather(gsent, gheld, gsend, grecv, 1, inner)
-    garrive()
-    gsent2[...] = jnp.sum(gheld[...], axis=0)
-    garrive2, gdepart2 = gather(gsent2, gheld2, gsend2, grecv2, inner, n // inner)
+    gsent[...] = jnp.broadcast_to(total, gsent.shape)
+    gheld[me] = total
+    for to in ("far", "near", "side", "own"):
+        start3(to, 0, size - 1 if to == "own" else size)
+    start2("side", 0, size)
+    start2("own", 0, size - 1)
+    landed[me] = back[me]
 
     late_phase = phase_of(1, late, home, late_edges, 2 * n, 0, False)
     rest_phase = phase_of(0, rest, home, [], 2 * n, 0, False)
-    for origin in (plane,) + others:
+    for origin in ("own", "side", "near", "far"):
         arrive2(origin)
     x = jnp.concatenate([landed[:, 0], landed[:, 1]], 0)
     x = turn(x, 1, late, home, late_phase, False)
@@ -686,19 +663,26 @@
     for bit in (1, 2):
         x = swap_bits(x, g - 2 + bit, bit)
     out_ref[...] = x.reshape(16 * n, 128)
-    garrive2()
-    grads_ref[...] = jnp.sum(gheld2[...], axis=0)
+    for origin in ("own", "side", "near", "far"):
+        arrive3(origin)
+    grads_ref[...] = jnp.sum(gheld[...], axis=0)
     depart1()
     depart2()
-    gdepart()
-    gdepart2()
-
-
-def finish(bra_ref, sums_ref, out_ref, grads_ref, sem):
-    copy = pltpu.make_async_copy(bra_ref, out_ref, sem)
-    copy.start()
-    grads_ref[...] = sums_ref[:, : grads_ref.shape[1]]
-    copy.wait()
+    depart3()
+
+
+def finish(bra_ref, sums_ref, out_ref, grads_ref, picked, sems):
+    picked[...] = sums_ref[pl.ds(0, picked.shape[0]), pl.ds(0, picked.shape[1])]
+    pieces = sems.shape[0] - 1
+    rows = out_ref.shape[0] // pieces
+    copies = [pltpu.make_async_copy(picked, grads_ref, sems.at[pieces])]
+    for k in range(pieces):
+        part = pl.ds(k * rows, rows)
+        copies.append(pltpu.make_async_copy(bra_ref.at[part], out_ref.at[part], sems.at[k]))
+    for copy in copies:
+        copy.start()
+    for copy in copies:
+        copy.wait()
 
 
 def by_exchange(ket_state, observable, angles, gate_kinds):
@@ -711,8 +695,6 @@
     vmem = pl.BlockSpec(memory_space=pltpu.VMEM)
     smem = pl.BlockSpec(memory_space=pltpu.SMEM)
     hbm = pl.BlockSpec(memory_space=pltpu.HBM)
-    inner = 1 << n.bit_length() // 2
-    outer = n // inner
     f32 = jnp.float32
     dma = pltpu.SemaphoreType.DMA
     bra, sums = pl.pallas_call(
@@ -730,18 +712,12 @@
             pltpu.VMEM((n, 3, 8, 128), f32),
             pltpu.VMEM((n, 2, 8, 128), f32),
             pltpu.VMEM((n, 2, 8, 128), f32),
-            pltpu.VMEM((layers, 128), f32),
-            pltpu.VMEM((inner, layers, 128), f32),
-            pltpu.VMEM((layers, 128), f32),
-            pltpu.VMEM((outer, layers, 128), f32),
+            pltpu.VMEM((n, layers, 128), f32),
+            pltpu.VMEM((n, layers, 128), f32),
             pltpu.SemaphoreType.REGULAR((PLANES,)),
-            dma,
-            dma((PLANES,)),
-            dma,
-            dma((PLANES,)),
         ]
-        + [dma((size,)) for size in (inner, inner, outer, outer, 2)]
-        + [pltpu.VMEM((layers, 128, 256), f32)],
+        + [dma((PLANES,))] * 6
+        + [dma((2,)), pltpu.VMEM((layers, 128, 256), f32)],
         compiler_params=pltpu.CompilerParams(
             collective_id=0, has_side_effects=True
         ),
@@ -753,8 +729,8 @@
             jax.ShapeDtypeStruct((layers, kind_count), f32),
         ),
         in_specs=[vmem, vmem],
-        out_specs=(hbm, vmem),
-        scratch_shapes=[dma],
+        out_specs=(hbm, hbm),
+        scratch_shapes=[pltpu.VMEM((layers, kind_count), f32), dma((5,))],
         compiler_params=pltpu.CompilerParams(vmem_limit_bytes=1 << 20),
     )(*(pltpu.with_memory_space_constraint(x, pltpu.VMEM) for x in (bra, sums)))
     bra_state = out.reshape(rows, 2, 128).transpose(1, 0, 2).reshape(2, amp_count)

time: 28.6 us -> 27.4 us (0.958)
  Pallas kernels: 27.8 us -> 26.6 us
    pallas_call x1, Pallas kernels: 26.5 us -> 25.9 us  [by_exchange(): pl.pallas_call(functools.partial(kernel, n, qubits), out_shape=(pltpu.VME...]
    pallas_call x1, Pallas kernels: 1.27 us -> 0.74 us  [by_exchange(): pl.pallas_call(finish, out_shape=(jax.ShapeDtypeStruct((2 * rows, 128), f...]
where the time goes in v2:
time: 27.4 us; the launch traced here: 27.2 us
  Pallas kernels  26.6 us (97%)
  between operations  0.64 us (2%)
    pallas_call x1, Pallas kernels, by_exchange(): pl.pallas_call(functools.partial(kernel, n, qubits), out_shape=(pltpu.VME...  25.9 us
    pallas_call x1, Pallas kernels, by_exchange(): pl.pallas_call(finish, out_shape=(jax.ShapeDtypeStruct((2 * rows, 128), f...  0.74 us

profile of v2, /device:TPU:0, one launch (start us, length us, event | category | flops | bytes accessed | tf_op | source)
XLA Modules:
  0.0 27.2 jit_solution(16851332195313687831)
XLA Ops:
  0.6 25.9 %shard_map.59 = (f32[512,128]{1,0:T(8,128)S(1)}, f32[2,128]{1,0:T(2,128)S(1)}) custom-call(f32[2,3]{1,0:T(2,128)} %angles.1, s32[2,32]{1,0:T(2,128)} %kinds.1, f32[512,128]{1,0:T(8,128)} %bitcast.11, f32[256,128]{1,0:T(8,128)} %bitcast.12), custom_call_target="tpu_custom_call" | custom-call | tf_op jit(solution)/shard_map/pallas_call | solution.py:700
  26.5 0.7 %shard_map.60 = (f32[512,128]{1,0:T(8,128)}, f32[2,3]{1,0:T(2,128)}) custom-call(f32[512,128]{1,0:T(8,128)S(1)} %get-tuple-element.6.bra_ref, f32[2,128]{1,0:T(2,128)S(1)} %get-tuple-element.7.sums_ref), custom_call_target="tpu_custom_call" | custom-call | tf_op jit(solution)/shard_map/pallas_call | solution.py:725

commit v3 on v2

--- a/solution.py
+++ b/solution.py
@@ -460,8 +460,8 @@
 
 def kernel(
     n, qubits, angles, kinds, ket_ref, obs_ref, out_ref, grads_ref,
-    ket_in, obs_in, sent, held, back, landed, gsent, gheld,
-    flag, send1, recv1, send2, recv2, gsend, grecv, load, wide,
+    ket_in, obs_in, sent, held, back, landed,
+    flag, send1, recv1, send2, recv2, load, wide, flips, begun,
 ):
     me = lax.axis_index("amp")
     g = n.bit_length() - 1
@@ -502,28 +502,28 @@
     value = ket_in[...].reshape(2 * n, 8, 128)
     for bit in (1, 2):
         value = swap_bits(value, g - 2 + bit, bit)
-    sent[:, 0] = value[:n]
-    sent[:, 1] = value[n:]
+    sent[:, pl.ds(0, 8)] = value[:n]
+    sent[:, pl.ds(8, 8)] = value[n:]
     value = obs_in[...].reshape(n, 8, 128)
     for major, bit in ((g - 2, 0), (g - 1, 2)):
         value = swap_bits(value, major, bit)
-    sent[:, 2] = jnp.stack([value[:half], value[half:]], axis=1).reshape(n, 8, 128)
+    sent[:, pl.ds(16, 8)] = jnp.stack([value[:half], value[half:]], axis=1).reshape(n, 8, 128)
 
     pl.semaphore_wait(barrier, size - 1 + len(others))
     for other in others:
         pl.semaphore_signal(flag.at[plane], inc=1, device_id=(other * size + place,), device_id_type=MESH)
 
-    def exchange(source, target, send, recv, tiles):
-        def part(ref, block, to):
-            return ref.at[block, pl.ds(0, tiles[to])] if tiles else ref.at[block]
+    def exchange(source, target, send, recv, rows):
+        def part(ref, block):
+            return ref.at[block, pl.ds(0, rows)]
 
         def start(to, lower, upper):
             @pl.loop(lower, upper)
             def _(k):
                 block = planes[to] * size + inside(size - 1 - k)
                 pltpu.make_async_remote_copy(
-                    src_ref=part(source, block, to),
-                    dst_ref=part(target, me, to),
+                    src_ref=part(source, block),
+                    dst_ref=part(target, me),
                     send_sem=send.at[planes[to]],
                     recv_sem=recv.at[plane],
                     device_id=(block,),
@@ -533,8 +533,8 @@
         def many(to):
             blocks = pl.ds(planes[to] * size, size - 1 if to == "own" else size)
             return pltpu.make_async_remote_copy(
-                src_ref=part(source, blocks, to),
-                dst_ref=part(target, blocks, to),
+                src_ref=part(source, blocks),
+                dst_ref=part(target, blocks),
                 send_sem=send.at[planes[to]],
                 recv_sem=recv.at[planes[to]],
                 device_id=(me,),
@@ -543,9 +543,8 @@
 
         return start, lambda to: many(to).wait_recv(), lambda: [many(to).wait_send() for to in planes]
 
-    start1, arrive1, depart1 = exchange(sent, held, send1, recv1, dict.fromkeys(planes, 3))
-    start2, arrive2, depart2 = exchange(back, landed, send2, recv2, dict.fromkeys(planes, 2))
-    start3, arrive3, depart3 = exchange(gsent, gheld, gsend, grecv, None)
+    start1, arrive1, depart1 = exchange(sent, held, send1, recv1, 24)
+    start2, arrive2, depart2 = exchange(back, landed, send2, recv2, 17)
     start1("far", size - 1, size)
     start1("near", size - 1, size)
     start1("own", 0, size - 1)
@@ -610,12 +609,12 @@
         for q in chosen:
             if not (by_matrix and place[q][0] == LANE):
                 x = y_gate(x, place[q], coefs[l][q][0], coefs[l][q][1])
-        return phase[0] * x + phase[1] * other_part(x)
+        return x if phase is None else phase[0] * x + phase[1] * other_part(x)
 
     sign, _ = phases(home, qubits, every, 2 * n, me, 0)
     phase = phase_of(1, local, home, every, 2 * n, 0, True)
-    ket = jnp.concatenate([sent[:, 0], sent[:, 1]], 0) * sign
-    obs = sent[:, 2]
+    ket = jnp.concatenate([sent[:, pl.ds(0, 8)], sent[:, pl.ds(8, 8)]], 0) * sign
+    obs = sent[:, pl.ds(16, 8)]
     bra = scale * jnp.concatenate([weights(obs, 0), weights(obs, 1)], 0) * ket
     add_terms(1, local, home, bra, ket)
     ket, bra = (turn(x, 1, local, home, phase) for x in (ket, bra))
@@ -624,55 +623,71 @@
     ready_phase = phase_of(0, ready, away, [], n, 0, True)
     signs = [phases(away, qubits, every, n, me, chunk)[0] for chunk in range(2)]
     mid_phases = [phase_of(1, here, away, early_edges, n, chunk, True) for chunk in range(2)]
+    for chunk in range(2):
+        flips[chunk] = signs[chunk]
+    inner = size.bit_length() - 1
+    wide_here = [q for q in here if away[q][0] == MAJOR and away[q][1] >= inner]
+    slim_here = [q for q in here if q not in wide_here]
     for origin in ("own", "side", "near", "far"):
         arrive1(origin)
-    states = []
+        blocks = pl.ds(planes[origin] * size, size)
+        for chunk in range(2):
+            ket = held[blocks, pl.ds(8 * chunk, 8)] * flips[chunk, blocks]
+            bra = scale * weights(held[blocks, pl.ds(16, 8)], chunk) * ket
+            add_terms(1, [q for q in outer if q in slim_here], away, bra, ket)
+            begun[chunk, 0, blocks] = ket
+            begun[chunk, 1, blocks] = bra
+            begun[chunk, 2, blocks] = turn(ket, 1, slim_here, away, None)
+            begun[chunk, 3, blocks] = turn(bra, 1, slim_here, away, None)
     for chunk in range(2):
-        ket = held[:, chunk] * signs[chunk]
-        bra = scale * weights(held[:, 2], chunk) * ket
-        bra_mid = turn(bra, 1, here, away, mid_phases[chunk])
-        back[:, chunk] = turn(bra_mid, 0, ready, away, ready_phase)
-        states.append((ket, bra, bra_mid))
+        phase = mid_phases[chunk]
+        bra = turn(begun[chunk, 3], 1, wide_here, away, phase, False)
+        back[:, pl.ds(8 * chunk, 8)] = turn(bra, 0, ready, away, ready_phase)
+        add_terms(1, [q for q in outer if q in wide_here], away, begun[chunk, 1], begun[chunk, 0])
+        ket = turn(begun[chunk, 2], 1, wide_here, away, phase, False)
+        add_terms(0, [local[-1]] + outer + [0], away, bra, ket)
+    spot = [lax.broadcasted_iota(jnp.int32, (8, 128), d) for d in range(2)]
+    total = jnp.zeros((8, 128), jnp.float32)
+    for l in range(layers):
+        for k in range(kind_count):
+            row = jnp.sum(sums[l][k], axis=0, keepdims=True)
+            total = total + jnp.where(spot[0] == l * kind_count + k, row, 0.0)
+    total = jnp.sum(total, axis=1, keepdims=True)
+    total = jnp.sum(jnp.where(spot[0] == spot[1], total, 0.0), axis=0, keepdims=True)
+    back[:, pl.ds(16, 1)] = jnp.broadcast_to(total, (n, 1, 128))
+
     start2("far", 0, size)
     start2("near", 0, size)
-    for chunk, (ket, bra, bra_mid) in enumerate(states):
-        add_terms(1, outer, away, bra, ket)
-        ket = turn(ket, 1, here, away, mid_phases[chunk])
-        add_terms(0, [local[-1]] + outer + [0], away, bra_mid, ket)
-
-    at = [lax.broadcasted_iota(jnp.int32, (layers, 128), d) for d in range(2)]
-    total = jnp.zeros((layers, 128), jnp.float32)
-    for l in range(layers):
-        for k in range(kind_count):
-            total = total + jnp.where((at[0] == l) & (at[1] == k), jnp.sum(sums[l][k]), 0.0)
-    gsent[...] = jnp.broadcast_to(total, gsent.shape)
-    gheld[me] = total
-    for to in ("far", "near", "side", "own"):
-        start3(to, 0, size - 1 if to == "own" else size)
     start2("side", 0, size)
     start2("own", 0, size - 1)
     landed[me] = back[me]
 
     late_phase = phase_of(1, late, home, late_edges, 2 * n, 0, False)
     rest_phase = phase_of(0, rest, home, [], 2 * n, 0, False)
+    wide_late = [q for q in late if inner <= home[q][1] < g]
+    slim = {q: (MAJOR, min(home[q][1], inner)) for q in late if q not in wide_late}
     for origin in ("own", "side", "near", "far"):
         arrive2(origin)
-    x = jnp.concatenate([landed[:, 0], landed[:, 1]], 0)
-    x = turn(x, 1, late, home, late_phase, False)
+        blocks = pl.ds(planes[origin] * size, size)
+        x = jnp.concatenate([landed[blocks, pl.ds(0, 8)], landed[blocks, pl.ds(8, 8)]], 0)
+        x = turn(x, 1, list(slim), slim, None, False)
+        begun[0, 0, blocks] = x[:size]
+        begun[1, 0, blocks] = x[size:]
+    x = jnp.concatenate([begun[0, 0], begun[1, 0]], 0)
+    x = turn(x, 1, wide_late, home, late_phase, False)
     x = turn(x, 0, rest, home, rest_phase, False)
     for bit in (1, 2):
         x = swap_bits(x, g - 2 + bit, bit)
     out_ref[...] = x.reshape(16 * n, 128)
-    for origin in ("own", "side", "near", "far"):
-        arrive3(origin)
-    grads_ref[...] = jnp.sum(gheld[...], axis=0)
+    grads_ref[...] = jnp.sum(landed[:, pl.ds(16, 1)], axis=0)
     depart1()
     depart2()
-    depart3()
 
 
 def finish(bra_ref, sums_ref, out_ref, grads_ref, picked, sems):
-    picked[...] = sums_ref[pl.ds(0, picked.shape[0]), pl.ds(0, picked.shape[1])]
+    layers, kind_count = picked.shape
+    for l in range(layers):
+        picked[pl.ds(l, 1), :] = sums_ref[:, pl.ds(l * kind_count, kind_count)]
     pieces = sems.shape[0] - 1
     rows = out_ref.shape[0] // pieces
     copies = [pltpu.make_async_copy(picked, grads_ref, sems.at[pieces])]
@@ -701,23 +716,21 @@
         functools.partial(kernel, n, qubits),
         out_shape=(
             pltpu.VMEM((2 * rows, 128), f32),
-            pltpu.VMEM((layers, 128), f32),
+            pltpu.VMEM((1, 128), f32),
         ),
         in_specs=[smem, smem, hbm, hbm],
         out_specs=(vmem, vmem),
         scratch_shapes=[
             pltpu.VMEM((2 * rows, 128), f32),
             pltpu.VMEM((rows, 128), f32),
-            pltpu.VMEM((n, 3, 8, 128), f32),
-            pltpu.VMEM((n, 3, 8, 128), f32),
-            pltpu.VMEM((n, 2, 8, 128), f32),
-            pltpu.VMEM((n, 2, 8, 128), f32),
-            pltpu.VMEM((n, layers, 128), f32),
-            pltpu.VMEM((n, layers, 128), f32),
+        ]
+        + [pltpu.VMEM((n, 24, 128), f32)] * 4
+        + [
             pltpu.SemaphoreType.REGULAR((PLANES,)),
         ]
-        + [dma((PLANES,))] * 6
-        + [dma((2,)), pltpu.VMEM((layers, 128, 256), f32)],
+        + [dma((PLANES,))] * 4
+        + [dma((2,)), pltpu.VMEM((layers, 128, 256), f32)]
+        + [pltpu.VMEM((2, n, 8, 128), f32), pltpu.VMEM((2, 4, n, 8, 128), f32)],
         compiler_params=pltpu.CompilerParams(
             collective_id=0, has_side_effects=True
         ),

time: 27.4 us -> 26.1 us (0.953)
  Pallas kernels: 26.6 us -> 25.3 us
    pallas_call x1, Pallas kernels: 25.9 us -> 24.5 us  [by_exchange(): pl.pallas_call(functools.partial(kernel, n, qubits), out_shape=(pltpu.VME...]
where the time goes in v3:
time: 26.1 us; the launch traced here: 25.9 us
  Pallas kernels  25.3 us (97%)
  between operations  0.64 us (2%)
    pallas_call x1, Pallas kernels, by_exchange(): pl.pallas_call(functools.partial(kernel, n, qubits), out_shape=(pltpu.VME...  24.5 us
    pallas_call x1, Pallas kernels, by_exchange(): pl.pallas_call(finish, out_shape=(jax.ShapeDtypeStruct((2 * rows, 128), f...  0.81 us

profile of v3, /device:TPU:0, one launch (start us, length us, event | category | flops | bytes accessed | tf_op | source)
XLA Modules:
  0.0 25.9 jit_solution(4462770211913826698)
XLA Ops:
  0.6 24.5 %shard_map.59 = (f32[512,128]{1,0:T(8,128)S(1)}, f32[1,128]{1,0:T(1,128)S(1)}) custom-call(f32[2,3]{1,0:T(2,128)} %angles.1, s32[2,32]{1,0:T(2,128)} %kinds.1, f32[512,128]{1,0:T(8,128)} %bitcast.11, f32[256,128]{1,0:T(8,128)} %bitcast.12), custom_call_target="tpu_custom_call" | custom-call | tf_op jit(solution)/shard_map/pallas_call | solution.py:715
  25.1 0.8 %shard_map.60 = (f32[512,128]{1,0:T(8,128)}, f32[2,3]{1,0:T(2,128)}) custom-call(f32[512,128]{1,0:T(8,128)S(1)} %get-tuple-element.6.bra_ref, f32[1,128]{1,0:T(1,128)S(1)} %get-tuple-element.7.sums_ref), custom_call_target="tpu_custom_call" | custom-call | tf_op jit(solution)/shard_map/pallas_call | solution.py:738

commit v4 on v3

--- a/solution.py
+++ b/solution.py
@@ -359,6 +359,30 @@
     return cy * x + (sy * minor_sign(axis, bit)) * partner(x, axis, bit)
 
 
+def major_gates(x, gates, phase):
+    tiles = [x[i : i + 1] for i in range(x.shape[0])]
+    split = (len(gates) + 1) // 2 if len(gates) > 3 else len(gates)
+    passes = [p for p in (gates[:split], gates[split:]) if p]
+    for number, some in enumerate(passes):
+        spread = sum(1 << bit for bit, _, _ in some)
+        for base in range(len(tiles)):
+            if base & spread:
+                continue
+            group = [base]
+            for bit, _, _ in some:
+                group = group + [i + (1 << bit) for i in group]
+            for bit, cy, sy in some:
+                for i in group:
+                    if not i >> bit & 1:
+                        j = i + (1 << bit)
+                        a, b = tiles[i], tiles[j]
+                        tiles[i], tiles[j] = cy * a + sy * b, cy * b - sy * a
+            if phase is not None and number == len(passes) - 1:
+                for i in group:
+                    tiles[i] = phase[0][i : i + 1] * tiles[i] + phase[1][i : i + 1] * other_part(tiles[i])
+    return jnp.concatenate(tiles, 0)
+
+
 def lane_matrix(coefs):
     at = [lax.broadcasted_iota(jnp.int32, (128, 128), d) for d in range(2)]
     re, im = None, None
@@ -504,14 +528,14 @@
         value = swap_bits(value, g - 2 + bit, bit)
     sent[:, pl.ds(0, 8)] = value[:n]
     sent[:, pl.ds(8, 8)] = value[n:]
+    pl.semaphore_wait(barrier, size - 1 + len(others))
+    for other in others:
+        pl.semaphore_signal(flag.at[plane], inc=1, device_id=(other * size + place,), device_id_type=MESH)
     value = obs_in[...].reshape(n, 8, 128)
     for major, bit in ((g - 2, 0), (g - 1, 2)):
         value = swap_bits(value, major, bit)
     sent[:, pl.ds(16, 8)] = jnp.stack([value[:half], value[half:]], axis=1).reshape(n, 8, 128)
 
-    pl.semaphore_wait(barrier, size - 1 + len(others))
-    for other in others:
-        pl.semaphore_signal(flag.at[plane], inc=1, device_id=(other * size + place,), device_id_type=MESH)
 
     def exchange(source, target, send, recv, rows):
         def part(ref, block):
@@ -606,10 +630,13 @@
     def turn(x, l, chosen, place, phase, by_matrix=True):
         if by_matrix:
             x = turn_lanes(x, wide.at[l])
+        majors = []
         for q in chosen:
-            if not (by_matrix and place[q][0] == LANE):
+            if place[q][0] == MAJOR:
+                majors.append((place[q][1], coefs[l][q][0], coefs[l][q][1]))
+            elif not (by_matrix and place[q][0] == LANE):
                 x = y_gate(x, place[q], coefs[l][q][0], coefs[l][q][1])
-        return x if phase is None else phase[0] * x + phase[1] * other_part(x)
+        return major_gates(x, majors, phase)
 
     sign, _ = phases(home, qubits, every, 2 * n, me, 0)
     phase = phase_of(1, local, home, every, 2 * n, 0, True)

time: 26.1 us -> 26 us (level)
  no operation moved by 1% of the time
where the time goes in v4:
time: 26 us; the launch traced here: 25.8 us
  Pallas kernels  25.2 us (97%)
  between operations  0.64 us (2%)
    pallas_call x1, Pallas kernels, by_exchange(): pl.pallas_call(functools.partial(kernel, n, qubits), out_shape=(pltpu.VME...  24.4 us
    pallas_call x1, Pallas kernels, by_exchange(): pl.pallas_call(finish, out_shape=(jax.ShapeDtypeStruct((2 * rows, 128), f...  0.81 us

profile of v4, /device:TPU:0, one launch (start us, length us, event | category | flops | bytes accessed | tf_op | source)
XLA Modules:
  0.0 25.8 jit_solution(3377582322604571962)
XLA Ops:
  0.6 24.4 %shard_map.59 = (f32[512,128]{1,0:T(8,128)S(1)}, f32[1,128]{1,0:T(1,128)S(1)}) custom-call(f32[2,3]{1,0:T(2,128)} %angles.1, s32[2,32]{1,0:T(2,128)} %kinds.1, f32[512,128]{1,0:T(8,128)} %bitcast.11, f32[256,128]{1,0:T(8,128)} %bitcast.12), custom_call_target="tpu_custom_call" | custom-call | tf_op jit(solution)/shard_map/pallas_call | solution.py:742
  25.0 0.8 %shard_map.60 = (f32[512,128]{1,0:T(8,128)}, f32[2,3]{1,0:T(2,128)}) custom-call(f32[512,128]{1,0:T(8,128)S(1)} %get-tuple-element.6.bra_ref, f32[1,128]{1,0:T(1,128)S(1)} %get-tuple-element.7.sums_ref), custom_call_target="tpu_custom_call" | custom-call | tf_op jit(solution)/shard_map/pallas_call | solution.py:765

commit v5 on v4

--- a/solution.py
+++ b/solution.py
@@ -531,7 +531,7 @@
     pl.semaphore_wait(barrier, size - 1 + len(others))
     for other in others:
         pl.semaphore_signal(flag.at[plane], inc=1, device_id=(other * size + place,), device_id_type=MESH)
-    value = obs_in[...].reshape(n, 8, 128)
+    value = scale * obs_in[...].reshape(n, 8, 128)
     for major, bit in ((g - 2, 0), (g - 1, 2)):
         value = swap_bits(value, major, bit)
     sent[:, pl.ds(16, 8)] = jnp.stack([value[:half], value[half:]], axis=1).reshape(n, 8, 128)
@@ -642,7 +642,7 @@
     phase = phase_of(1, local, home, every, 2 * n, 0, True)
     ket = jnp.concatenate([sent[:, pl.ds(0, 8)], sent[:, pl.ds(8, 8)]], 0) * sign
     obs = sent[:, pl.ds(16, 8)]
-    bra = scale * jnp.concatenate([weights(obs, 0), weights(obs, 1)], 0) * ket
+    bra = jnp.concatenate([weights(obs, 0), weights(obs, 1)], 0) * ket
     add_terms(1, local, home, bra, ket)
     ket, bra = (turn(x, 1, local, home, phase) for x in (ket, bra))
     add_terms(0, local[1:-1], home, bra, ket)
@@ -660,7 +660,7 @@
         blocks = pl.ds(planes[origin] * size, size)
         for chunk in range(2):
             ket = held[blocks, pl.ds(8 * chunk, 8)] * flips[chunk, blocks]
-            bra = scale * weights(held[blocks, pl.ds(16, 8)], chunk) * ket
+            bra = weights(held[blocks, pl.ds(16, 8)], chunk) * ket
             add_terms(1, [q for q in outer if q in slim_here], away, bra, ket)
             begun[chunk, 0, blocks] = ket
             begun[chunk, 1, blocks] = bra

time: 26 us -> 26 us (level)
  no operation moved by 1% of the time
where the time goes in v5:
time: 26 us; the launch traced here: 25.8 us
  Pallas kernels  25.2 us (97%)
  between operations  0.64 us (2%)
    pallas_call x1, Pallas kernels, by_exchange(): pl.pallas_call(functools.partial(kernel, n, qubits), out_shape=(pltpu.VME...  24.4 us
    pallas_call x1, Pallas kernels, by_exchange(): pl.pallas_call(finish, out_shape=(jax.ShapeDtypeStruct((2 * rows, 128), f...  0.81 us

profile of v5, /device:TPU:0, one launch (start us, length us, event | category | flops | bytes accessed | tf_op | source)
XLA Modules:
  0.0 25.8 jit_solution(9463559300060156882)
XLA Ops:
  0.6 24.4 %shard_map.59 = (f32[512,128]{1,0:T(8,128)S(1)}, f32[1,128]{1,0:T(1,128)S(1)}) custom-call(f32[2,3]{1,0:T(2,128)} %angles.1, s32[2,32]{1,0:T(2,128)} %kinds.1, f32[512,128]{1,0:T(8,128)} %bitcast.11, f32[256,128]{1,0:T(8,128)} %bitcast.12), custom_call_target="tpu_custom_call" | custom-call | tf_op jit(solution)/shard_map/pallas_call | solution.py:742
  25.0 0.8 %shard_map.60 = (f32[512,128]{1,0:T(8,128)}, f32[2,3]{1,0:T(2,128)}) custom-call(f32[512,128]{1,0:T(8,128)S(1)} %get-tuple-element.6.bra_ref, f32[1,128]{1,0:T(1,128)S(1)} %get-tuple-element.7.sums_ref), custom_call_target="tpu_custom_call" | custom-call | tf_op jit(solution)/shard_map/pallas_call | solution.py:765
